TPU v7x, 32 devices: a whole 2x2x4 slice. The times are simulated.
32 devices in a mesh: grp: 8 (over y, x, core), wide: 4 (over z).
Axes of the slice: x: 2, y: 2, z: 4, core: 2. Of those that a mesh axis runs over, the one named last changes fastest.
Arguments:
- gradient: bfloat16 [8, 4, 16, 4096], P('grp', 'wide'), may hold values from -6 to 6
- residual: float32 [8, 4, 16, 4096], P('grp', 'wide'), may hold values from -4 to 4
- selected: int32 [8, 4, 4, 32], P('grp', 'wide'), may hold values from 0 to 127, as said below
- counts: int32 [8, 4, 4], P('grp', 'wide'), may hold values from 1 to 32, as said below
Outputs:
- update: float32 [4, 4, 4096], P('wide')
- new_residual: float32 [8, 4, 16, 4096], P('grp', 'wide')
Inputs may be any that keep to these rules, and one draw needn't show every extreme that they name: `selected`: for each device and shard, 32 distinct block numbers of that shard; entries at or past the count are ignored. `counts`: one shard has 32 on every device; every device has at most one other shard at 32, the rest at most 16.
All inputs are finite; a program needn't handle non-finite values.
Results may differ from a plain program's by a relative error of at most 0.0003.
Values sent between devices are 32-bit elements; how exact they have to be, the bound alone decides.
No kernel may reach another device: no remote copies, remote signals or barrier semaphores. Data moves between devices by JAX's collectives and lax.ppermute only.
A program may use at most 64 MiB of HBM per device.

v0:
```python
import jax
import jax.numpy as jnp
from jax import lax
from jax.sharding import PartitionSpec as P


def body(gradient, residual, selected, counts):
    shards = lax.axis_size("wide")
    groups = lax.axis_size("grp")
    rows = gradient.shape[2]
    width = gradient.shape[3]
    block_len = 128
    own_rows = rows // shards
    own_blocks = own_rows * width // block_len
    slots = selected.shape[3]
    accumulated = gradient[0, 0].astype(jnp.float32) + residual[0, 0]
    blocks = accumulated.reshape(shards, own_blocks, block_len)
    picks = selected[0, 0]
    used = counts[0, 0]
    block_ids = jnp.arange(own_blocks, dtype=jnp.int32)
    one_hot = (picks[:, :, None] == block_ids).astype(jnp.float32)
    valid = (jnp.arange(slots, dtype=jnp.int32)[None, :] < used[:, None]).astype(jnp.float32)
    mask = jnp.einsum("wk,wkb->wb", valid, one_hot, precision=lax.Precision.HIGHEST)
    new_residual = (blocks * (1.0 - mask[..., None])).reshape(1, 1, rows, width)
    chosen = (
        jnp.einsum("wkb,wbc->wkc", one_hot, blocks, precision=lax.Precision.HIGHEST)
        * valid[..., None]
    )
    chosen_ids = picks.astype(jnp.float32)
    arrived, arrived_ids = (
        lax.all_to_all(chosen, "wide", split_axis=0, concat_axis=0, tiled=True),
        lax.all_to_all(chosen_ids, "wide", split_axis=0, concat_axis=0, tiled=True),
    )
    arrived_hot = (arrived_ids[:, :, None] == block_ids.astype(jnp.float32)).astype(jnp.float32)
    partial_sum = jnp.einsum("skb,skc->bc", arrived_hot, arrived, precision=lax.Precision.HIGHEST)
    summed = lax.psum(partial_sum, "grp")
    update = (summed / groups).reshape(1, own_rows, width)
    return (update, new_residual)


def solution(mesh):
    return jax.shard_map(
        body,
        mesh=mesh,
        in_specs=(
            P("grp", "wide", None, None),
            P("grp", "wide", None, None),
            P("grp", "wide", None, None),
            P("grp", "wide", None),
        ),
        out_specs=(P("wide", None, None), P("grp", "wide", None, None)),
        check_vma=False,
    )
```

profile of v0, /device:TPU:0, one launch (start us, length us, event | category | flops | bytes accessed | tf_op | source)
XLA Modules:
  0.0 91.7 jit_solution(3083365458631421438)
XLA Ops:
  7.2 1.3 %convert_element_type.35 = f32[1,1,4,32]{3,2,1,0:T(4,128)} convert(s32[1,1,4,32]{3,2,1,0:T(4,128)} %param.6) | non-fusion elementwise | flops 128 | bytes 1024 | tf_op jit(solution)/shard_map/convert_element_type | solution.py:29
  8.4 6.3 %all-to-all-start = ((f32[4,1,32]{2,1,0:T(1,128)}), f32[4,1,32]{2,1,0:T(1,128)S(1)}, u32[]{:S(2)}, u32[]{:S(2)}) async-start(f32[4,1,32]{2,1,0:T(1,128)} %bitcast.1), calls=%async_computation | async-start | bytes 4096 | tf_op jit(solution)/shard_map/all_to_all | solution.py:32
  14.8 0.0 copy-start.3
  14.8 0.7 copy-done.3
  15.4 0.1 fusion.8
  15.5 0.0 copy-start.2
  15.5 0.7 copy-done.2
  16.2 0.2 fusion
  16.4 0.1 mul.21
  16.5 0.0 copy-start
  16.5 0.0 copy-start.1
  16.5 0.1 mul.22
  16.6 0.9 copy-done
  17.5 0.0 copy-done.1
  17.5 0.7 fusion.9
  18.3 0.9 convolution_multiply_fusion
  19.2 1.1 %all-to-all-done = f32[4,1,32]{2,1,0:T(1,128)S(1)} async-done(((f32[4,1,32]{2,1,0:T(1,128)}), f32[4,1,32]{2,1,0:T(1,128)S(1)}, u32[]{:S(2)}, u32[]{:S(2)}) %all-to-all-start) | async-done | bytes 544 | tf_op jit(solution)/shard_map/all_to_all | solution.py:32
  20.3 4.0 %all-to-all-start.1 = ((f32[4,32,128]{2,1,0:T(8,128)}), f32[4,32,128]{2,1,0:T(8,128)S(1)}, u32[]{:S(2)}, u32[]{:S(2)}) async-start(f32[4,32,128]{2,1,0:T(8,128)} %convolution_multiply_fusion), calls=%async_computation.1 | async-start | bytes 131072 | tf_op jit(solution)/shard_map/all_to_all | solution.py:31
  24.3 0.0 all-reduce.2.cloned.1.call-start
  24.3 5.7 %all-to-all-done.1 = f32[4,32,128]{2,1,0:T(8,128)S(1)} async-done(((f32[4,32,128]{2,1,0:T(8,128)}), f32[4,32,128]{2,1,0:T(8,128)S(1)}, u32[]{:S(2)}, u32[]{:S(2)}) %all-to-all-start.1) | async-done | bytes 65568 | tf_op jit(solution)/shard_map/all_to_all | solution.py:31
  30.1 0.9 %convolution_bitcast_fusion = f32[128,128]{1,0:T(8,128)} fusion(f32[4,32,128]{2,1,0:T(8,128)S(1)} %all-to-all-done.1, f32[128]{0:T(128)S(1)} %iota_convert_fusion, f32[4,32]{1,0:T(4,128)S(1)} %bitcast.16), kind=kOutput, calls=%fused_computation | convolution fusion | flops 25182208 | bytes 132096 | tf_op jit(solution)/shard_map/skb,skc->bc/dot_general | solution.py:35
  31.0 0.0 all-reduce.2.cloned.1.call-update
  31.0 52.4 %all-reduce.2.cloned.1.call-done = f32[128,128]{1,0:T(8,128)} async-done(((f32[128,128]{1,0:T(8,128)}), f32[128,128]{1,0:T(8,128)}) %all-reduce.2.cloned.1.call-update) | async-done | bytes 65552 | tf_op jit(solution)/shard_map/psum | solution.py:36
  83.4 0.8 broadcast_multiply_fusion
  84.2 0.7 reshape.63
  (3 shorter events, 0.1 us)
Async XLA Ops:
  8.4 11.9 %all-to-all-start = ((f32[4,1,32]{2,1,0:T(1,128)}), f32[4,1,32]{2,1,0:T(1,128)S(1)}, u32[]{:S(2)}, u32[]{:S(2)}) async-start(f32[4,1,32]{2,1,0:T(1,128)} %bitcast.1), calls=%async_computation | async-start | bytes 4096 | tf_op jit(solution)/shard_map/all_to_all | solution.py:32
  14.8 0.7 copy-start.3
  15.5 0.7 copy-start.2
  16.5 1.0 %copy-start = (f32[1,1,16,4096]{3,2,1,0:T(8,128)S(1)}, f32[1,1,16,4096]{3,2,1,0:T(8,128)}, u32[]{:S(2)}) copy-start(f32[1,1,16,4096]{3,2,1,0:T(8,128)} %param.5) | copy-start | bytes 786436
  16.5 1.0 %copy-start.1 = (bf16[1,1,16,4096]{3,2,1,0:T(8,128)(2,1)S(1)}, bf16[1,1,16,4096]{3,2,1,0:T(8,128)(2,1)}, u32[]{:S(2)}) copy-start(bf16[1,1,16,4096]{3,2,1,0:T(8,128)(2,1)} %param.4) | copy-start | bytes 393220
  20.3 9.7 %all-to-all-start.1 = ((f32[4,32,128]{2,1,0:T(8,128)}), f32[4,32,128]{2,1,0:T(8,128)S(1)}, u32[]{:S(2)}, u32[]{:S(2)}) async-start(f32[4,32,128]{2,1,0:T(8,128)} %convolution_multiply_fusion), calls=%async_computation.1 | async-start | bytes 131072 | tf_op jit(solution)/shard_map/all_to_all | solution.py:31
  24.3 59.1 %all-reduce.2.cloned.1.call-start = ((), (), s32[]{:S(2)}) async-start(), calls=%async_computation.2 | async-start | bytes 131072 | tf_op jit(solution)/shard_map/psum | solution.py:36
Sparse Core Ops, SparseCore 0:
  31.1 52.2 all-reduce.1
where the time goes:
time: 92.1 us; the launch traced here: 91.7 us
  waiting for transfers between devices  59.3 us (64%)
  between operations  14.1 us (15%)
  starting transfers between devices  10.3 us (11%)
  local copies, waits for them, and re-layouts  3.13 us (3%)
  other arithmetic  2.93 us (3%)
  matrix products  2.05 us (2%)
    psum x1, waiting for transfers between devices, body(): summed = lax.psum(partial_sum, 'grp')  52.4 us
    all_to_all x1, starting transfers between devices, body(): lax.all_to_all(chosen_ids, 'wide', split_axis=0, concat_axis=0, tiled=True)  6.35 us
    all_to_all x1, waiting for transfers between devices, body(): lax.all_to_all(chosen, 'wide', split_axis=0, concat_axis=0, tiled=True)  5.74 us
    all_to_all x1, starting transfers between devices, body(): lax.all_to_all(chosen, 'wide', split_axis=0, concat_axis=0, tiled=True)  3.96 us
    unnamed x8, local copies, waits for them, and re-layouts  2.25 us
  transfers between devices with their start and end apart: 3, of which 3 were waited for; matrix products, arithmetic and copies ran while one was open for 2% of the time, Pallas kernels for 0%

commit v1 on v0

--- a/solution.py
+++ b/solution.py
@@ -33,7 +33,8 @@
     )
     arrived_hot = (arrived_ids[:, :, None] == block_ids.astype(jnp.float32)).astype(jnp.float32)
     partial_sum = jnp.einsum("skb,skc->bc", arrived_hot, arrived, precision=lax.Precision.HIGHEST)
-    summed = lax.psum(partial_sum, "grp")
+    levels_all_write = lambda axis_id, payload: jnp.sum(lax.all_gather(payload, axis_id), 0)
+    summed = levels_all_write("grp", partial_sum)
     update = (summed / groups).reshape(1, own_rows, width)
     return (update, new_residual)
 

time: 92.1 us -> 34.8 us (0.38)
  waiting for transfers between devices: 59.3 us -> 6.87 us
  between operations: 14.1 us -> 0.68 us
  blocking collectives: 0 us -> 9.86 us
    psum x1 -> x0, waiting for transfers between devices: 52.4 us -> none  [body(): summed = lax.psum(partial_sum, 'grp')]
    all_gather x0 -> x1, blocking collectives: none -> 9.86 us  [body(): lax.all_gather(payload, axis_id)]
  transfers between devices with their start and end apart: 3 -> 2, of which waited for: 3 -> 2; matrix products, arithmetic and copies ran while one was open for 2% -> 6% of each run, Pallas kernels for 0% -> 0%
where the time goes in v1:
time: 34.8 us; the launch traced here: 34.4 us
  starting transfers between devices  10.3 us (30%)
  blocking collectives  9.86 us (28%)
  waiting for transfers between devices  6.87 us (20%)
  local copies, waits for them, and re-layouts  3.13 us (9%)
  other arithmetic  2.13 us (6%)
  matrix products  1.42 us (4%)
  between operations  0.68 us (2%)
    all_gather x1, blocking collectives, body(): lax.all_gather(payload, axis_id)  9.86 us
    all_to_all x1, starting transfers between devices, body(): lax.all_to_all(chosen_ids, 'wide', split_axis=0, concat_axis=0, tiled=True)  6.35 us
    all_to_all x1, waiting for transfers between devices, body(): lax.all_to_all(chosen, 'wide', split_axis=0, concat_axis=0, tiled=True)  5.74 us
    all_to_all x1, starting transfers between devices, body(): lax.all_to_all(chosen, 'wide', split_axis=0, concat_axis=0, tiled=True)  3.96 us
    unnamed x8, local copies, waits for them, and re-layouts  2.25 us
    convert_element_type x1, other arithmetic, body(): chosen_ids = picks.astype(jnp.float32)  1.27 us
    all_to_all x1, waiting for transfers between devices, body(): lax.all_to_all(chosen_ids, 'wide', split_axis=0, concat_axis=0, tiled=True)  1.13 us
    dot_general x1, matrix products, body(): jnp.einsum('wkb,wbc->wkc', one_hot, blocks, precision=lax.Precision.HIGHEST)  0.91 us
  transfers between devices with their start and end apart: 2, of which 2 were waited for; matrix products, arithmetic and copies ran while one was open for 6% of the time, Pallas kernels for 0%

profile of v1, /device:TPU:0, one launch (start us, length us, event | category | flops | bytes accessed | tf_op | source)
XLA Modules:
  0.0 34.4 jit_solution(12081509573842560310)
XLA Ops:
  0.6 1.3 %convert_element_type.35 = f32[1,1,4,32]{3,2,1,0:T(4,128)} convert(s32[1,1,4,32]{3,2,1,0:T(4,128)} %param.6) | non-fusion elementwise | flops 128 | bytes 1024 | tf_op jit(solution)/shard_map/convert_element_type | solution.py:29
  1.9 6.3 %all-to-all-start = ((f32[4,1,32]{2,1,0:T(1,128)}), f32[4,1,32]{2,1,0:T(1,128)S(1)}, u32[]{:S(2)}, u32[]{:S(2)}) async-start(f32[4,1,32]{2,1,0:T(1,128)} %bitcast.1), calls=%async_computation | async-start | bytes 4096 | tf_op jit(solution)/shard_map/all_to_all | solution.py:32
  8.2 0.0 copy-start.3
  8.2 0.7 %copy-done.3 = s32[1,1,4]{2,1,0:T(1,128)S(1)} copy-done((s32[1,1,4]{2,1,0:T(1,128)S(1)}, s32[1,1,4]{2,1,0:T(1,128)}, u32[]{:S(2)}) %copy-start.3) | copy-done | bytes 40
  8.9 0.1 fusion.8
  9.0 0.0 copy-start.2
  9.0 0.7 %copy-done.2 = s32[1,1,4,32]{3,2,1,0:T(4,128)S(1)} copy-done((s32[1,1,4,32]{3,2,1,0:T(4,128)S(1)}, s32[1,1,4,32]{3,2,1,0:T(4,128)}, u32[]{:S(2)}) %copy-start.2) | copy-done | bytes 536
  9.7 0.2 fusion
  9.9 0.1 mul.21
  10.0 0.0 copy-start
  10.0 0.0 copy-start.1
  10.0 0.1 mul.22
  10.1 0.9 %copy-done = f32[1,1,16,4096]{3,2,1,0:T(8,128)S(1)} copy-done((f32[1,1,16,4096]{3,2,1,0:T(8,128)S(1)}, f32[1,1,16,4096]{3,2,1,0:T(8,128)}, u32[]{:S(2)}) %copy-start) | copy-done | bytes 262168
  11.0 0.0 copy-done.1
  11.0 0.7 %fusion.9 = (f32[1,1,16,4096]{3,2,1,0:T(8,128)}, f32[1,1,16,4096]{3,2,1,0:T(8,128)S(1)}) fusion(f32[1,1,16,4096]{3,2,1,0:T(8,128)S(1)} %mul.22, f32[1,1,16,4096]{3,2,1,0:T(8,128)S(1)} %copy-done, bf16[1,1,16,4096]{3,2,1,0:T(8,128)(2,1)S(1)} %copy-done.1), kind=kLoop, calls=%fused_computation.17 | loop fusion | flops 196608 | bytes 1179648 | tf_op jit(solution)/shard_map/mul | solution.py:24
  11.8 0.9 %convolution_multiply_fusion = f32[4,32,128]{2,1,0:T(8,128)} fusion(f32[4,128,128]{2,1,0:T(8,128)S(1)} %add.9, f32[4,32]{1,0:T(4,128)S(1)} %get-tuple-element.4, s32[4,32]{1,0:T(4,128)S(1)} %bitcast.20), kind=kOutput, calls=%fused_computation.1 | convolution fusion | flops 25198592 | bytes 328704 | tf_op jit(solution)/shard_map/wkb,wbc->wkc/dot_general | solution.py:26
  12.7 1.1 %all-to-all-done = f32[4,1,32]{2,1,0:T(1,128)S(1)} async-done(((f32[4,1,32]{2,1,0:T(1,128)}), f32[4,1,32]{2,1,0:T(1,128)S(1)}, u32[]{:S(2)}, u32[]{:S(2)}) %all-to-all-start) | async-done | bytes 544 | tf_op jit(solution)/shard_map/all_to_all | solution.py:32
  13.8 4.0 %all-to-all-start.1 = ((f32[4,32,128]{2,1,0:T(8,128)}), f32[4,32,128]{2,1,0:T(8,128)S(1)}, u32[]{:S(2)}, u32[]{:S(2)}) async-start(f32[4,32,128]{2,1,0:T(8,128)} %convolution_multiply_fusion), calls=%async_computation.1 | async-start | bytes 131072 | tf_op jit(solution)/shard_map/all_to_all | solution.py:31
  17.8 5.7 %all-to-all-done.1 = f32[4,32,128]{2,1,0:T(8,128)S(1)} async-done(((f32[4,32,128]{2,1,0:T(8,128)}), f32[4,32,128]{2,1,0:T(8,128)S(1)}, u32[]{:S(2)}, u32[]{:S(2)}) %all-to-all-start.1) | async-done | bytes 65568 | tf_op jit(solution)/shard_map/all_to_all | solution.py:31
  23.5 0.3 convolution_bitcast_fusion
  23.8 9.9 %all-gather = f32[1024,128]{1,0:T(8,128)S(1)} all-gather(f32[128,128]{1,0:T(8,128)S(1)} %convolution_bitcast_fusion), channel_id=2, replica_groups=mesh['grp'=8,'wide'=4] {'grp'}, dimensions={0}, use_global_device_ids=true | all-gather | bytes 589824 | tf_op jit(solution)/shard_map/all_gather | solution.py:36
  33.8 0.7 %div.10 = f32[1,4,4096]{2,1,0:T(4,128)} reshape(f32[128,128]{1,0:T(8,128)S(1)} %broadcast_multiply_fusion) | data formatting | bytes 131072 | tf_op jit(solution)/shard_map/div | solution.py:38
  (5 shorter events, 0.1 us)
Async XLA Ops:
  1.9 11.9 %all-to-all-start = ((f32[4,1,32]{2,1,0:T(1,128)}), f32[4,1,32]{2,1,0:T(1,128)S(1)}, u32[]{:S(2)}, u32[]{:S(2)}) async-start(f32[4,1,32]{2,1,0:T(1,128)} %bitcast.1), calls=%async_computation | async-start | bytes 4096 | tf_op jit(solution)/shard_map/all_to_all | solution.py:32
  8.2 0.7 %copy-start.3 = (s32[1,1,4]{2,1,0:T(1,128)S(1)}, s32[1,1,4]{2,1,0:T(1,128)}, u32[]{:S(2)}) copy-start(s32[1,1,4]{2,1,0:T(1,128)} %param.7) | copy-start | bytes 52
  9.0 0.7 %copy-start.2 = (s32[1,1,4,32]{3,2,1,0:T(4,128)S(1)}, s32[1,1,4,32]{3,2,1,0:T(4,128)}, u32[]{:S(2)}) copy-start(s32[1,1,4,32]{3,2,1,0:T(4,128)} %param.6) | copy-start | bytes 1540
  10.0 1.0 %copy-start = (f32[1,1,16,4096]{3,2,1,0:T(8,128)S(1)}, f32[1,1,16,4096]{3,2,1,0:T(8,128)}, u32[]{:S(2)}) copy-start(f32[1,1,16,4096]{3,2,1,0:T(8,128)} %param.5) | copy-start | bytes 786436
  10.0 1.0 %copy-start.1 = (bf16[1,1,16,4096]{3,2,1,0:T(8,128)(2,1)S(1)}, bf16[1,1,16,4096]{3,2,1,0:T(8,128)(2,1)}, u32[]{:S(2)}) copy-start(bf16[1,1,16,4096]{3,2,1,0:T(8,128)(2,1)} %param.4) | copy-start | bytes 393220
  13.8 9.7 %all-to-all-start.1 = ((f32[4,32,128]{2,1,0:T(8,128)}), f32[4,32,128]{2,1,0:T(8,128)S(1)}, u32[]{:S(2)}, u32[]{:S(2)}) async-start(f32[4,32,128]{2,1,0:T(8,128)} %convolution_multiply_fusion), calls=%async_computation.1 | async-start | bytes 131072 | tf_op jit(solution)/shard_map/all_to_all | solution.py:31
